TPU v7x, 32 devices: a whole 2x2x4 slice. The times are simulated.
32 devices in a mesh: group: 4 (over x, core), dp: 8 (over z, y).
Axes of the slice: x: 2, y: 2, z: 4, core: 2. Of those that a mesh axis runs over, the one named last changes fastest.
Arguments:
- param_units: int32 [6], replicated, may hold values from 1 to 144, 384 in all
- first_moment: bfloat16 [3072, 7168], P(('group', 'dp')), may hold values from -1.796875 to 1.796875
- second_moment: bfloat16 [3072, 7168], P(('group', 'dp')), may hold values from 0.0099487305 to 1
- grad_parts: bfloat16 [4, 3072, 7168], P('group', 'dp'), may hold values from -17 to 17, as said below
- weights: bfloat16 [3072, 7168], P('dp', 'group'), may hold values from -6 to 6
Outputs:
- new_first: bfloat16 [3072, 7168], P('dp', 'group')
- new_second: bfloat16 [3072, 7168], P('dp', 'group')
- direction: float32 [3072, 7168], P('dp', 'group')
- grad_rms: float32 [], replicated
Inputs may be any that keep to these rules, and one draw needn't show every extreme that they name: `param_units`: 6 counts, each from 1 to 144, summing to 384; the largest is exactly 144. `grad_parts`: entries of one group's partial have scales between exp(-3.2) and exp(1.2) that vary with the block of 32 rows and with the column; entries lie within -17 and 17.
All inputs are finite; a program needn't handle non-finite values.
Results may differ from a plain program's by a relative error of at most 0.012.
Values may be sent and summed in bfloat16 or wider, within the bound.
A program may use at most 128 MiB of HBM per device.

v0:
```python
import jax
import jax.numpy as jnp
from jax import lax
from jax.sharding import PartitionSpec as P

beta_first = 0.9
beta_second = 0.95
epsilon = 1e-08
decay_weight = 0.1


def owner_of(positions, bounds):
    return jnp.sum(positions[..., None] >= bounds, axis=-1)


def lookup(choose, table):
    return jnp.sum(jnp.where(choose, table, 0), axis=-1)


def local(param_units, first_moment, second_moment, grad_parts, weights):
    groups = lax.axis_size("group")
    shards = lax.axis_size("dp")
    rows_local = weights.shape[0]
    width_part = weights.shape[1]
    width_full = grad_parts.shape[2]
    zero_rows = first_moment.shape[0]
    row_blocks = zero_rows // shards
    param_count = param_units.shape[0]
    capacity = rows_local // shards + param_count
    offsets = jnp.cumsum(param_units) - param_units
    slot_count = (param_units + shards - 1) // shards
    slot_base = jnp.cumsum(slot_count) - slot_count
    param_range = jnp.arange(param_count, dtype=jnp.int32)
    lane_index = lax.axis_index("dp")
    summed = lax.psum_scatter(
        grad_parts.astype(jnp.float32).astype(jnp.bfloat16),
        "group",
        scatter_dimension=2,
        tiled=True,
    ).astype(jnp.float32)[0]
    square_sum = lax.psum(jnp.sum(summed * summed), ("group", "dp"))
    grad_rms = jnp.sqrt(square_sum / float(rows_local * shards * width_full))
    clipped = summed / jnp.maximum(grad_rms, 1.0)
    arranged_first = (
        first_moment.reshape(row_blocks, shards, groups, width_part)
        .swapaxes(1, 2)
        .reshape(row_blocks, groups * shards, width_part)
    )
    arranged_second = (
        second_moment.reshape(row_blocks, shards, groups, width_part)
        .swapaxes(1, 2)
        .reshape(row_blocks, groups * shards, width_part)
    )
    spread_first, spread_second = (
        lax.all_to_all(arranged_first, ("group", "dp"), split_axis=1, concat_axis=1, tiled=True),
        lax.all_to_all(arranged_second, ("group", "dp"), split_axis=1, concat_axis=1, tiled=True),
    )
    middle_first = spread_first.reshape(rows_local, width_part)
    middle_second = spread_second.reshape(rows_local, width_part)
    targets = jnp.arange(shards, dtype=jnp.int32)[:, None]
    slot_index = jnp.arange(capacity, dtype=jnp.int32)[None, :]
    slot_owner = owner_of(slot_index, slot_base + slot_count)
    choose_slot = slot_owner[..., None] == param_range
    slot_units = lookup(choose_slot, param_units)
    slot_offsets = lookup(choose_slot, offsets)
    slot_first = lookup(choose_slot, slot_base)
    within = jnp.mod(lane_index - targets * slot_units, shards) + shards * (slot_index - slot_first)
    usable = (slot_owner < param_count) & (within < slot_units)
    zero_row = shards * slot_offsets + targets * slot_units + within
    source_block = zero_row // zero_rows
    inner_block = zero_row % zero_rows // shards
    located = (inner_block * groups + source_block // shards) * shards + source_block % shards
    located = jnp.where(usable, located, 0)
    outgoing_first = jnp.where(usable[..., None], jnp.take(middle_first, located, axis=0), 0)
    outgoing_second = jnp.where(usable[..., None], jnp.take(middle_second, located, axis=0), 0)
    received_first, received_second = (
        lax.all_to_all(outgoing_first, "dp", split_axis=0, concat_axis=0, tiled=True),
        lax.all_to_all(outgoing_second, "dp", split_axis=0, concat_axis=0, tiled=True),
    )
    local_rows = jnp.arange(rows_local, dtype=jnp.int32)
    row_owner = owner_of(local_rows, offsets + param_units)
    choose_rows = row_owner[:, None] == param_range
    row_units = lookup(choose_rows, param_units)
    row_offsets = lookup(choose_rows, offsets)
    row_base = lookup(choose_rows, slot_base)
    within_rows = local_rows - row_offsets
    source_lane = jnp.mod(lane_index * row_units + within_rows, shards)
    picked = source_lane * capacity + row_base + within_rows // shards
    first_rows = jnp.take(
        received_first.reshape(shards * capacity, width_part), picked, axis=0
    ).astype(jnp.float32)
    second_rows = jnp.take(
        received_second.reshape(shards * capacity, width_part), picked, axis=0
    ).astype(jnp.float32)
    first_new = beta_first * first_rows + (1.0 - beta_first) * clipped
    second_new = beta_second * second_rows + (1.0 - beta_second) * clipped * clipped
    direction = first_new / (jnp.sqrt(second_new) + epsilon) + decay_weight * weights.astype(
        jnp.float32
    )
    return (first_new.astype(jnp.bfloat16), second_new.astype(jnp.bfloat16), direction, grad_rms)


def solution(mesh):
    in_specs = (
        P(),
        P(("group", "dp"), None),
        P(("group", "dp"), None),
        P("group", "dp", None),
        P("dp", "group"),
    )
    out_specs = (P("dp", "group"), P("dp", "group"), P("dp", "group"), P())
    return jax.shard_map(local, mesh=mesh, in_specs=in_specs, out_specs=out_specs, check_vma=False)
```

profile of v0, /device:TPU:0, one launch (start us, length us, event | category | flops | bytes accessed | tf_op | source)
XLA Modules:
  0.0 260.0 jit_solution(3243418974896525700)
XLA Ops:
  7.2 3.4 %copy.13 = bf16[12,8,4,1792]{3,0,1,2:T(8,128)(2,1)} copy(bf16[12,8,4,1792]{3,1,2,0:T(8,128)(2,1)} %bitcast.34) | data formatting | bytes 2752512 | tf_op jit(solution)/shard_map/reshape | solution.py:45
  10.5 7.3 %all-to-all-start = ((bf16[12,32,1792]{2,0,1:T(8,128)(2,1)}), bf16[12,32,1792]{2,0,1:T(8,128)(2,1)S(1)}, u32[]{:S(2)}, u32[]{:S(2)}) async-start(bf16[12,32,1792]{2,0,1:T(8,128)(2,1)} %bitcast.33), calls=%async_computation | async-start | bytes 3670016 | tf_op jit(solution)/shard_map/all_to_all | solution.py:55
  17.9 0.0 copy-start.2
  17.9 0.0 reduce-scatter.2.cloned.1.call-start
  17.9 0.7 reduce-scatter.2.cloned.1.call-update
  18.6 0.6 copy-done.2
  19.2 2.0 copy.15
  21.2 41.1 %all-to-all-done = bf16[12,32,1792]{2,0,1:T(8,128)(2,1)S(1)} async-done(((bf16[12,32,1792]{2,0,1:T(8,128)(2,1)}), bf16[12,32,1792]{2,0,1:T(8,128)(2,1)S(1)}, u32[]{:S(2)}, u32[]{:S(2)}) %all-to-all-start) | async-done | bytes 1376288 | tf_op jit(solution)/shard_map/all_to_all | solution.py:55
  62.3 0.0 copy-start.3
  62.3 3.6 %all-to-all-start.2 = ((bf16[12,32,1792]{2,0,1:T(8,128)(2,1)}), bf16[12,32,1792]{2,0,1:T(8,128)(2,1)}, u32[]{:S(2)}, u32[]{:S(2)}) async-start(bf16[12,32,1792]{2,0,1:T(8,128)(2,1)} %bitcast.32), calls=%async_computation.3 | async-start | bytes 3670016 | tf_op jit(solution)/shard_map/all_to_all | solution.py:56
  65.9 0.0 copy-done.3
  65.9 0.2 reduce-window.17
  66.1 0.2 reduce-window.16
  66.3 0.1 fusion.17
  66.4 0.1 select_reduce_fusion.5
  66.5 0.1 reshape.412
  66.7 0.4 copy.14
  67.1 2.4 gather_fusion
  69.5 1.4 reshape.415
  70.9 39.5 %all-to-all-done.2 = bf16[12,32,1792]{2,0,1:T(8,128)(2,1)} async-done(((bf16[12,32,1792]{2,0,1:T(8,128)(2,1)}), bf16[12,32,1792]{2,0,1:T(8,128)(2,1)}, u32[]{:S(2)}, u32[]{:S(2)}) %all-to-all-start.2) | async-done | bytes 1376288 | tf_op jit(solution)/shard_map/all_to_all | solution.py:56
  110.3 1.9 copy.16
  112.2 2.4 gather_fusion.2
  114.6 0.0 copy-start
  114.6 1.4 reshape.421
  116.0 0.6 copy-done
  116.6 3.0 %select_select_fusion = (bf16[8,54,1792]{2,1,0:T(8,128)(2,1)S(1)}, bf16[8,54,1792]{2,1,0:T(8,128)(2,1)}) fusion(bf16[8,54,1792]{2,1,0:T(8,128)(2,1)} %reshape.421, pred[8,54]{1,0:T(8,128)(4,1)S(1)} %get-tuple-element.20, pred[8,54]{1,0:T(8,128)(4,1)S(1)} %get-tuple-element.19, bf16[8,54,1792]{2,1,0:T(8,128)(2,1)S(1)} %copy-done), kind=kLoop, calls=%fused_computation.12 | loop fusion | flops 3096576 | bytes 6194016 | tf_op jit(solution)/shard_map/jit(_where)/select_n | solution.py:75
  119.6 41.6 %all_to_all.20 = bf16[8,54,1792]{2,1,0:T(8,128)(2,1)} all-to-all(bf16[8,54,1792]{2,1,0:T(8,128)(2,1)S(1)} %get-tuple-element.17), channel_id=1, replica_groups=mesh['group'=4,'dp'=8] {'dp'}, dimensions={0} | all-to-all | bytes 3096576 | tf_op jit(solution)/shard_map/all_to_all | solution.py:78
  161.3 3.6 %all-to-all-start.1 = ((bf16[8,54,1792]{2,1,0:T(8,128)(2,1)}), bf16[8,54,1792]{2,1,0:T(8,128)(2,1)S(1)}, u32[]{:S(2)}, u32[]{:S(2)}) async-start(bf16[8,54,1792]{2,1,0:T(8,128)(2,1)} %get-tuple-element.18), calls=%async_computation.1 | async-start | bytes 3211264 | tf_op jit(solution)/shard_map/all_to_all | solution.py:77
  164.9 0.1 convert_reduce_fusion
  164.9 0.1 select_reduce_fusion.1
  165.1 1.6 reshape.373
  166.7 3.0 %gather_fusion.3 = bf16[384,1792]{1,0:T(8,128)(2,1)} fusion(bf16[432,1792]{1,0:T(8,128)(2,1)S(1)} %reshape.373, s32[1024]{0:T(1024)S(1)} %pad_clamp_fusion), kind=kCustom, calls=%fused_computation.3.clone | custom fusion | bytes 2754048 | tf_op jit(solution)/shard_map/jit(_take)/gather | solution.py:92
  169.7 32.1 %all-to-all-done.1 = bf16[8,54,1792]{2,1,0:T(8,128)(2,1)S(1)} async-done(((bf16[8,54,1792]{2,1,0:T(8,128)(2,1)}), bf16[8,54,1792]{2,1,0:T(8,128)(2,1)S(1)}, u32[]{:S(2)}, u32[]{:S(2)}) %all-to-all-start.1) | async-done | bytes 1548320 | tf_op jit(solution)/shard_map/all_to_all | solution.py:77
  201.8 0.4 reshape.369
  202.2 0.0 reduce-scatter.2.cloned.1.call-done
  202.3 2.7 %fusion = f32[]{:T(128)} fusion(bf16[1,384,1792]{2,1,0:T(8,128)(2,1)} %reduce-scatter.2.cloned.1.call-done), kind=kLoop, calls=%fused_computation.7 | loop fusion | flops 2064383 | bytes 1376260 | tf_op jit(solution)/shard_map/reduce_sum | solution.py:41
  204.9 0.0 copy-start.1
  204.9 3.0 %gather_fusion.1 = bf16[384,1792]{1,0:T(8,128)(2,1)} fusion(bf16[432,1792]{1,0:T(8,128)(2,1)S(1)} %reshape.369, s32[1024]{0:T(1024)S(1)} %pad_clamp_fusion), kind=kCustom, calls=%fused_computation.1.clone | custom fusion | bytes 2754048 | tf_op jit(solution)/shard_map/jit(_take)/gather | solution.py:89
  207.9 37.9 %psum.7 = f32[]{:T(128)} all-reduce(f32[]{:T(128)} %fusion), channel_id=1, replica_groups=mesh['group'=4,'dp'=8] {'group','dp'}, use_global_device_ids=true, to_apply=%region_12.15 | all-reduce | flops 1 | bytes 8 | tf_op jit(solution)/shard_map/psum | solution.py:41
  246.5 0.0 copy-done.1
  246.5 5.5 %multiply_add_fusion = (f32[384,1792]{1,0:T(8,128)}, bf16[384,1792]{1,0:T(8,128)(2,1)}, bf16[384,1792]{1,0:T(8,128)(2,1)}) fusion(bf16[384,1792]{1,0:T(8,128)(2,1)} %param.13, f32[]{:T(128)S(6)} %max.3, bf16[1,384,1792]{2,1,0:T(8,128)(2,1)} %reduce-scatter.2.cloned.1.call-done, bf16[384,1792]{1,0:T(8,128)(2,1)} %gather_fusion.1, ...), kind=kLoop, calls=%fused_computation.10 | loop fusion | flops 13762560 | bytes 11010436 | tf_op jit(solution)/shard_map/add | solution.py:97
  (9 shorter events, 0.1 us)
Async XLA Ops:
  10.5 51.8 %all-to-all-start = ((bf16[12,32,1792]{2,0,1:T(8,128)(2,1)}), bf16[12,32,1792]{2,0,1:T(8,128)(2,1)S(1)}, u32[]{:S(2)}, u32[]{:S(2)}) async-start(bf16[12,32,1792]{2,0,1:T(8,128)(2,1)} %bitcast.33), calls=%async_computation | async-start | bytes 3670016 | tf_op jit(solution)/shard_map/all_to_all | solution.py:55
  17.9 1.3 copy-start.2
  17.9 184.4 %reduce-scatter.2.cloned.1.call-start = ((), (), s32[]{:S(2)}) async-start(), calls=%async_computation.5 | async-start | bytes 6881280 | tf_op jit(solution)/shard_map/reduce_scatter | solution.py:35
  62.3 3.6 %copy-start.3 = (s32[6]{0:T(128)S(1)}, s32[6]{0:T(128)}, u32[]{:S(2)}) copy-start(s32[6]{0:T(128)} %param.9) | copy-start | bytes 76
  62.3 48.0 %all-to-all-start.2 = ((bf16[12,32,1792]{2,0,1:T(8,128)(2,1)}), bf16[12,32,1792]{2,0,1:T(8,128)(2,1)}, u32[]{:S(2)}, u32[]{:S(2)}) async-start(bf16[12,32,1792]{2,0,1:T(8,128)(2,1)} %bitcast.32), calls=%async_computation.3 | async-start | bytes 3670016 | tf_op jit(solution)/shard_map/all_to_all | solution.py:56
  114.6 2.0 copy-start
  161.3 40.5 %all-to-all-start.1 = ((bf16[8,54,1792]{2,1,0:T(8,128)(2,1)}), bf16[8,54,1792]{2,1,0:T(8,128)(2,1)S(1)}, u32[]{:S(2)}, u32[]{:S(2)}) async-start(bf16[8,54,1792]{2,1,0:T(8,128)(2,1)} %get-tuple-element.18), calls=%async_computation.1 | async-start | bytes 3211264 | tf_op jit(solution)/shard_map/all_to_all | solution.py:77
  204.9 41.6 %copy-start.1 = (bf16[384,1792]{1,0:T(8,128)(2,1)S(1)}, bf16[384,1792]{1,0:T(8,128)(2,1)}, u32[]{:S(2)}) copy-start(bf16[384,1792]{1,0:T(8,128)(2,1)} %gather_fusion.3) | copy-start | bytes 4128772
Sparse Core Ops, SparseCore 0:
  21.2 73.7 reduce-scatter.1
where the time goes:
time: 261 us; the launch traced here: 260 us
  waiting for transfers between devices  113 us (43%)
  blocking collectives  79.5 us (30%)
  local copies, waits for them, and re-layouts  24.5 us (9%)
  between operations  16 us (6%)
  starting transfers between devices  14.5 us (6%)
  other arithmetic  12.1 us (5%)
    all_to_all x1, blocking collectives, local(): lax.all_to_all(outgoing_second, 'dp', split_axis=0, concat_axis=0, tiled=...  41.6 us
    all_to_all x1, waiting for transfers between devices, local(): lax.all_to_all(arranged_first, ('group', 'dp'), split_axis=1, concat_axis...  41.1 us
    all_to_all x1, waiting for transfers between devices, local(): lax.all_to_all(arranged_second, ('group', 'dp'), split_axis=1, concat_axi...  39.5 us
    psum x1, blocking collectives, local(): square_sum = lax.psum(jnp.sum(summed * summed), ('group', 'dp'))  37.9 us
    all_to_all x1, waiting for transfers between devices, local(): lax.all_to_all(outgoing_first, 'dp', split_axis=0, concat_axis=0, tiled=T...  32.1 us
    all_to_all x1, starting transfers between devices, local(): lax.all_to_all(arranged_first, ('group', 'dp'), split_axis=1, concat_axis...  7.33 us
    add x1, other arithmetic, local(): first_new / (jnp.sqrt(second_new) + epsilon)  5.5 us
  transfers between devices with their start and end apart: 4, of which 3 were waited for; matrix products, arithmetic and copies ran while one was open for 8% of the time, Pallas kernels for 0%

commit v1 on v0

v1 whole, which is shorter than its diff:
```python
import functools

import jax
import jax.numpy as jnp
from jax import lax
from jax.experimental import pallas as pl
from jax.experimental.pallas import tpu as pltpu
from jax.sharding import PartitionSpec as P

beta_first = 0.9
beta_second = 0.95
epsilon = 1e-08
decay_weight = 0.1
LANES = 128


class Plan:
    def __init__(self, groups, shards, tiles):
        self.groups, self.shards, self.tiles = groups, shards, tiles
        self.full, self.rest = tiles // shards, tiles % shards
        self.slots = []
        for moment in range(2):
            self.slots += [(moment, turn) for turn in range(self.full)]
            if self.rest:
                self.slots.append((moment, self.full))

    def partial(self, slot):
        return self.slots[slot][1] == self.full

    def place(self, slot, group, lane):
        moment, turn = self.slots[slot]
        if turn < self.full:
            return turn * self.shards + lane, None
        shift = (self.shards // 2) * moment + (self.shards // 4) * lax.rem(group, 2)
        rank = lax.rem(lane + shift, self.shards)
        return self.full * self.shards + jnp.minimum(rank, self.rest - 1), rank < self.rest


def when(condition, body):
    if condition is None:
        body()
    else:
        pl.when(condition)(body)


def both(first, second):
    return second if first is None else first & second


def await_bytes(ref, sem):
    pltpu.make_async_copy(ref, ref, sem).wait()


def spread_kernel(plan, zero_rows, width_part, first_ref, second_ref, middle_ref, send_sem, recv_sem, own_sem):
    group, lane = lax.axis_index("group"), lax.axis_index("dp")
    groups, shards = plan.groups, plan.shards
    base = (group * shards + lane) * zero_rows
    for slot, (moment, _) in enumerate(plan.slots):
        source = (first_ref, second_ref)[moment]

        def send(step, carry, slot=slot, source=source):
            to_group = lax.rem(group + lax.rem(step, groups), groups)
            to_lane = lax.rem(lane + step // groups, shards)
            tile, exists = plan.place(slot, to_group, to_lane)
            column = pl.multiple_of(to_group * width_part + tile * LANES, LANES)

            def start():
                pltpu.make_async_remote_copy(
                    src_ref=source.at[:, pl.ds(column, LANES)],
                    dst_ref=middle_ref.at[slot, pl.ds(base, zero_rows), :],
                    send_sem=send_sem.at[slot],
                    recv_sem=recv_sem.at[slot],
                    device_id=(to_group, to_lane),
                    device_id_type=pl.DeviceIdType.MESH,
                ).start()

            when(exists, start)
            return carry

        tile, exists = plan.place(slot, group, lane)
        column = pl.multiple_of(group * width_part + tile * LANES, LANES)
        own = pltpu.make_async_copy(
            source.at[:, pl.ds(column, LANES)],
            middle_ref.at[slot, pl.ds(base, zero_rows), :],
            own_sem.at[slot],
        )
        when(exists, own.start)
        lax.fori_loop(1, groups * shards, send, 0)
    for slot in range(len(plan.slots)):
        tile, exists = plan.place(slot, group, lane)
        arrived = middle_ref.at[slot, pl.ds(0, (groups * shards - 1) * zero_rows), :]
        if exists is None:
            await_bytes(arrived, send_sem.at[slot])
        else:
            others = groups * plan.rest
            less = middle_ref.at[slot, pl.ds(0, (others - 1) * zero_rows), :]
            more = middle_ref.at[slot, pl.ds(0, others * zero_rows), :]
            pl.when(exists)(functools.partial(await_bytes, less, send_sem.at[slot]))
            pl.when(~exists)(functools.partial(await_bytes, more, send_sem.at[slot]))

        def finish(slot=slot, arrived=arrived):
            await_bytes(arrived, recv_sem.at[slot])
            await_bytes(middle_ref.at[slot, pl.ds(0, zero_rows), :], own_sem.at[slot])

        when(exists, finish)


def deliver_kernel(plan, rows_local, ordered_ref, first_ref, second_ref, send_sem, recv_sem, own_sem):
    group, lane = lax.axis_index("group"), lax.axis_index("dp")
    shards = plan.shards
    results = (first_ref, second_ref)
    for slot, (moment, _) in enumerate(plan.slots):
        tile, exists = plan.place(slot, group, lane)
        target = results[moment].at[:, pl.ds(pl.multiple_of(tile * LANES, LANES), LANES)]

        def start_slot(slot=slot, moment=moment, target=target):
            pltpu.make_async_copy(
                ordered_ref.at[slot, pl.ds(lane * rows_local, rows_local), :], target, own_sem.at[slot]
            ).start()

            def send(step, carry):
                to_lane = lax.rem(lane + step, shards)
                pltpu.make_async_remote_copy(
                    src_ref=ordered_ref.at[slot, pl.ds(to_lane * rows_local, rows_local), :],
                    dst_ref=target,
                    send_sem=send_sem.at[slot],
                    recv_sem=recv_sem.at[moment],
                    device_id=(group, to_lane),
                    device_id_type=pl.DeviceIdType.MESH,
                ).start()
                return carry

            lax.fori_loop(1, shards, send, 0)

        when(exists, start_slot)
    for slot, (moment, turn) in enumerate(plan.slots):
        tile, exists = plan.place(slot, group, lane)

        def finish_slot(slot=slot):
            await_bytes(ordered_ref.at[slot, pl.ds(0, (shards - 1) * rows_local), :], send_sem.at[slot])
            await_bytes(ordered_ref.at[slot, pl.ds(0, rows_local), :], own_sem.at[slot])

        when(exists, finish_slot)
        if slot + 1 == len(plan.slots) or plan.slots[slot + 1][0] != moment:
            result = results[moment]

            def arrive(own, result=result, moment=moment):
                await_bytes(result.at[:, pl.ds(0, (plan.tiles - own) * LANES)], recv_sem.at[moment])

            if exists is None:
                arrive(plan.full)
            else:
                pl.when(exists)(functools.partial(arrive, plan.full + 1))
                pl.when(~exists)(functools.partial(arrive, plan.full))


def local(param_units, first_moment, second_moment, grad_parts, weights):
    groups = lax.axis_size("group")
    shards = lax.axis_size("dp")
    rows_local, width_part = weights.shape
    width_full = grad_parts.shape[2]
    zero_rows = first_moment.shape[0]
    rows = rows_local * shards
    plan = Plan(groups, shards, width_part // LANES)
    slots = len(plan.slots)
    anywhere = pl.BlockSpec(memory_space=pl.ANY)
    in_vmem = pl.BlockSpec(memory_space=pltpu.VMEM)

    summed = lax.psum_scatter(
        grad_parts.astype(jnp.float32).astype(jnp.bfloat16),
        "group",
        scatter_dimension=2,
        tiled=True,
    ).astype(jnp.float32)[0]
    square_sum = lax.psum(jnp.sum(summed * summed), ("group", "dp"))
    grad_rms = jnp.sqrt(square_sum / float(rows * width_full))
    clipped = summed / jnp.maximum(grad_rms, 1.0)

    middle = pl.pallas_call(
        functools.partial(spread_kernel, plan, zero_rows, width_part),
        out_shape=jax.ShapeDtypeStruct((slots, rows, LANES), jnp.bfloat16),
        in_specs=[anywhere, anywhere],
        out_specs=anywhere,
        scratch_shapes=[pltpu.SemaphoreType.DMA((slots,))] * 3,
        compiler_params=pltpu.CompilerParams(has_side_effects=True),
        cost_estimate=pl.CostEstimate(flops=0, bytes_accessed=60_000_000, transcendentals=0),
        name="spread",
    )(first_moment, second_moment)

    offsets = jnp.cumsum(param_units) - param_units
    local_rows = jnp.arange(rows_local, dtype=jnp.int32)
    owners = jnp.sum(local_rows[:, None] >= (offsets + param_units)[None, :], axis=1)
    choose = owners[:, None] == jnp.arange(param_units.shape[0])[None, :]
    row_units = jnp.sum(jnp.where(choose, param_units, 0), axis=1)
    row_offsets = jnp.sum(jnp.where(choose, offsets, 0), axis=1)
    lanes = jnp.arange(shards, dtype=jnp.int32)[:, None]
    source = (shards * row_offsets + lanes * row_units + local_rows - row_offsets).reshape(rows)
    ordered = jnp.take(middle, source, axis=1, mode="clip")

    first_rows, second_rows = pl.pallas_call(
        functools.partial(deliver_kernel, plan, rows_local),
        out_shape=[jax.ShapeDtypeStruct((rows_local, width_part), jnp.bfloat16)] * 2,
        in_specs=[anywhere],
        out_specs=[in_vmem, in_vmem],
        scratch_shapes=[
            pltpu.SemaphoreType.DMA((slots,)),
            pltpu.SemaphoreType.DMA((2,)),
            pltpu.SemaphoreType.DMA((slots,)),
        ],
        compiler_params=pltpu.CompilerParams(has_side_effects=True),
        cost_estimate=pl.CostEstimate(flops=0, bytes_accessed=60_000_000, transcendentals=0),
        name="deliver",
    )(ordered)
    first_rows = first_rows.astype(jnp.float32)
    second_rows = second_rows.astype(jnp.float32)
    first_new = beta_first * first_rows + (1.0 - beta_first) * clipped
    second_new = beta_second * second_rows + (1.0 - beta_second) * clipped * clipped
    direction = first_new / (jnp.sqrt(second_new) + epsilon) + decay_weight * weights.astype(
        jnp.float32
    )
    return (first_new.astype(jnp.bfloat16), second_new.astype(jnp.bfloat16), direction, grad_rms)


def solution(mesh):
    in_specs = (
        P(),
        P(("group", "dp"), None),
        P(("group", "dp"), None),
        P("group", "dp", None),
        P("dp", "group"),
    )
    out_specs = (P("dp", "group"), P("dp", "group"), P("dp", "group"), P())
    return jax.shard_map(local, mesh=mesh, in_specs=in_specs, out_specs=out_specs, check_vma=False)
```

time: 261 us -> 234 us (0.90)
  Pallas kernels: 0 us -> 136 us
  waiting for transfers between devices: 113 us -> 0.68 us
  blocking collectives: 79.5 us -> 41.7 us
  starting transfers between devices: 14.5 us -> 0.04 us
  local copies, waits for them, and re-layouts: 24.5 us -> 30.2 us
  other arithmetic: 12.1 us -> 9.17 us
    pallas_call x0 -> x2, Pallas kernels: none -> 136 us  [the longest x1 69.6 us: local(): pl.pallas_call(functools.partial(spread_kernel, plan, zero_rows, width_pa...]
    all_to_all x3 -> x0, waiting for transfers between devices: 113 us -> none  [the longest x1 41.1 us: local(): lax.all_to_all(arranged_first, ('group', 'dp'), split_axis=1, concat_axis...]
    all_to_all x1 -> x0, blocking collectives: 41.6 us -> none  [local(): lax.all_to_all(outgoing_second, 'dp', split_axis=0, concat_axis=0, tiled=...]
    all_to_all x3 -> x0, starting transfers between devices: 14.5 us -> none  [the longest x1 7.33 us: local(): lax.all_to_all(arranged_first, ('group', 'dp'), split_axis=1, concat_axis...]
    gather x6 -> x2, local copies, waits for them, and re-layouts: 13.5 us -> 25.5 us  [local(): ordered = jnp.take(middle, source, axis=1, mode='clip')]
    reshape x4 -> x0, local copies, waits for them, and re-layouts: 7.42 us -> none  [the longest x1 3.36 us: local(): first_moment.reshape(row_blocks, shards, groups, width_part).swapaxes(1, 2)]
    pallas_call x0 -> x1, local copies, waits for them, and re-layouts: none -> 4.7 us  [local(): pl.pallas_call(functools.partial(spread_kernel, plan, zero_rows, width_pa...]
    psum x1, blocking collectives: 37.9 us -> 41.7 us  [local(): square_sum = lax.psum(jnp.sum(summed * summed), ('group', 'dp'))]
  transfers between devices with their start and end apart: 4 -> 1, of which waited for: 3 -> 0; matrix products, arithmetic and copies ran while one was open for 8% -> 13% of each run, Pallas kernels for 0% -> 30%
where the time goes in v1:
time: 234 us
  Pallas kernels  136 us (58%)
  blocking collectives  41.7 us (18%)
  local copies, waits for them, and re-layouts  30.2 us (13%)
  between operations  15.9 us (7%)
  other arithmetic  9.17 us (4%)
    pallas_call x1, Pallas kernels, local(): pl.pallas_call(functools.partial(spread_kernel, plan, zero_rows, width_pa...  69.6 us
    pallas_call x1, Pallas kernels, local(): pl.pallas_call(functools.partial(deliver_kernel, plan, rows_local), out_s...  66.6 us
    psum x1, blocking collectives, local(): square_sum = lax.psum(jnp.sum(summed * summed), ('group', 'dp'))  41.7 us
    gather x2, local copies, waits for them, and re-layouts, local(): ordered = jnp.take(middle, source, axis=1, mode='clip')  25.5 us
    add x1, other arithmetic, local(): first_new / (jnp.sqrt(second_new) + epsilon)  5.99 us
    pallas_call x1, local copies, waits for them, and re-layouts, local(): pl.pallas_call(functools.partial(spread_kernel, plan, zero_rows, width_pa...  4.7 us
  transfers between devices with their start and end apart: 1, of which 0 were waited for; matrix products, arithmetic and copies ran while one was open for 13% of the time, Pallas kernels for 30%

profile of v1, /device:TPU:0, one launch (start us, length us, event | category | flops | bytes accessed | tf_op | source)
XLA Modules:
  0.0 233.8 jit_solution(2862497734501523154)
XLA Ops:
  7.2 0.0 copy-start.2
  7.2 0.0 reduce-scatter.2.cloned.1.call-start
  7.2 0.7 reduce-scatter.2.cloned.1.call-update
  7.9 0.0 copy-done.2
  7.9 0.2 reduce-window.8
  8.1 0.1 convert_reduce_fusion
  8.2 0.1 select_reduce_fusion
  8.3 69.6 %spread.1 = bf16[4,3072,128]{2,1,0:T(8,128)(2,1)} custom-call(bf16[96,7168]{1,0:T(8,128)(2,1)} %first_ref.1, bf16[96,7168]{1,0:T(8,128)(2,1)} %second_ref.1), custom_call_target="tpu_custom_call" | custom-call | bytes 60000000 | tf_op jit(solution)/shard_map/spread/pallas_call | solution.py:179
  78.0 4.7 %copy.11 = bf16[4,3072,128]{2,0,1:T(4,128)(2,1)S(1)} copy(bf16[4,3072,128]{2,1,0:T(8,128)(2,1)} %spread.1) | data formatting | bytes 6291456 | tf_op jit(solution)/shard_map/spread/pallas_call | solution.py:179
  82.7 21.5 %gather_fusion = bf16[3072,4,128]{2,1,0:T(4,128)(2,1)} fusion(bf16[4,3072,128]{2,0,1:T(4,128)(2,1)S(1)} %copy.11, s32[3072]{0:T(1024)S(1)} %broadcast_clamp_fusion), kind=kCustom, calls=%fused_computation | custom fusion | bytes 6303744 | tf_op jit(solution)/shard_map/jit(_take)/gather | solution.py:198
  104.2 4.0 %copy.14 = bf16[3072,4,128]{2,0,1:T(8,128)(2,1)} copy(bf16[3072,4,128]{2,1,0:T(4,128)(2,1)} %gather_fusion) | data formatting | bytes 6291456 | tf_op jit(solution)/shard_map/jit(_take)/gather | solution.py:198
  108.1 0.0 copy-start.1
  108.1 0.0 reduce-scatter.2.cloned.1.call-done
  108.1 0.0 copy-start
  108.1 2.8 %fusion = f32[]{:T(128)} fusion(bf16[1,384,1792]{2,1,0:T(8,128)(2,1)} %reduce-scatter.2.cloned.1.call-done), kind=kLoop, calls=%fused_computation.5 | loop fusion | flops 2064383 | bytes 1376260 | tf_op jit(solution)/shard_map/reduce_sum | solution.py:175
  110.9 66.6 %deliver.1 = (bf16[384,1792]{1,0:T(8,128)(2,1)}, bf16[384,1792]{1,0:T(8,128)(2,1)}) custom-call(bf16[4,3072,128]{2,1,0:T(8,128)(2,1)} %bitcast.20), custom_call_target="tpu_custom_call" | custom-call | bytes 60000000 | tf_op jit(solution)/shard_map/deliver/pallas_call | solution.py:200
  177.5 41.7 %psum.7 = f32[]{:T(128)} all-reduce(f32[]{:T(128)} %fusion), channel_id=1, replica_groups=mesh['group'=4,'dp'=8] {'group','dp'}, use_global_device_ids=true, to_apply=%region_6.7 | all-reduce | flops 1 | bytes 8 | tf_op jit(solution)/shard_map/psum | solution.py:175
  219.9 0.0 copy-done.1
  219.9 0.0 copy-done
  219.9 6.0 %multiply_add_fusion = (f32[384,1792]{1,0:T(8,128)}, bf16[384,1792]{1,0:T(8,128)(2,1)}, bf16[384,1792]{1,0:T(8,128)(2,1)}) fusion(bf16[384,1792]{1,0:T(8,128)(2,1)S(1)} %copy-done.1, f32[]{:T(128)S(6)} %max.3, bf16[1,384,1792]{2,1,0:T(8,128)(2,1)S(1)} %copy-done, bf16[384,1792]{1,0:T(8,128)(2,1)} %get-tuple-element.6, bf16[384,1792]{1,0:T(8,128)(2,1)} %get-tuple-element.7), kind=kLoop, calls=%fused_computation.8 | loop fusion | flops 12386304 | bytes 11010052 | tf_op jit(solution)/shard_map/add | solution.py:218
  (5 shorter events, 0.0 us)
Async XLA Ops:
  7.2 0.7 copy-start.2
  7.2 101.0 %reduce-scatter.2.cloned.1.call-start = ((), (), s32[]{:S(2)}) async-start(), calls=%async_computation.1 | async-start | bytes 6881280 | tf_op jit(solution)/shard_map/reduce_scatter | solution.py:169
  108.1 111.7 %copy-start.1 = (bf16[384,1792]{1,0:T(8,128)(2,1)S(1)}, bf16[384,1792]{1,0:T(8,128)(2,1)}, u32[]{:S(2)}) copy-start(bf16[384,1792]{1,0:T(8,128)(2,1)} %param.9) | copy-start | bytes 4128772
  108.1 111.7 %copy-start = (bf16[1,384,1792]{2,1,0:T(8,128)(2,1)S(1)}, bf16[1,384,1792]{2,1,0:T(8,128)(2,1)}, u32[]{:S(2)}) copy-start(bf16[1,384,1792]{2,1,0:T(8,128)(2,1)} %reduce-scatter.2.cloned.1.call-done) | copy-start | bytes 4128772
Sparse Core Ops, SparseCore 0:
  10.5 70.2 reduce-scatter.1

commit v2 on v1

--- a/solution.py
+++ b/solution.py
@@ -12,6 +12,9 @@
 epsilon = 1e-08
 decay_weight = 0.1
 LANES = 128
+CHUNKS = 4
+BLOCK = 16
+RUN = 32
 
 
 class Plan:
@@ -51,10 +54,56 @@
     pltpu.make_async_copy(ref, ref, sem).wait()
 
 
-def spread_kernel(plan, zero_rows, width_part, first_ref, second_ref, middle_ref, send_sem, recv_sem, own_sem):
+def spread_kernel(
+    plan, zero_rows, width_part, first_ref, second_ref, grad_ref, middle_ref, summed_ref, square_ref,
+    pair_ref, mine_ref, across_ref, landed_ref,
+    send_sem, recv_sem, own_sem, load_sem, pair_send_sem, pair_recv_sem, across_send_sem, across_recv_sem,
+):
     group, lane = lax.axis_index("group"), lax.axis_index("dp")
     groups, shards = plan.groups, plan.shards
     base = (group * shards + lane) * zero_rows
+    rows_local = grad_ref.shape[1]
+    chunk = rows_local // CHUNKS
+    core = lax.rem(group, 2)
+    beside, opposite = group + 1 - 2 * core, lax.rem(group + 2, groups)
+
+    def quarter(owner, rows):
+        return grad_ref.at[0, rows, pl.ds(pl.multiple_of(owner * width_part, LANES), width_part)]
+
+    def part(place):
+        return pl.ds(place * chunk, chunk)
+
+    def load(place, piece):
+        return pltpu.make_async_copy(
+            quarter((opposite, group)[place], part(piece)),
+            mine_ref.at[place, part(piece), :],
+            load_sem.at[place, piece],
+        )
+
+    def hand(place, piece):
+        return pltpu.make_async_remote_copy(
+            src_ref=quarter((lax.rem(beside + 2, groups), beside)[place], part(piece)),
+            dst_ref=pair_ref.at[place, part(piece), :],
+            send_sem=pair_send_sem.at[place, piece],
+            recv_sem=pair_recv_sem.at[place, piece],
+            device_id=(beside, lane),
+            device_id_type=pl.DeviceIdType.MESH,
+        )
+
+    def cross(piece):
+        return pltpu.make_async_remote_copy(
+            src_ref=across_ref.at[part(piece), :],
+            dst_ref=landed_ref.at[part(piece), :],
+            send_sem=across_send_sem.at[piece],
+            recv_sem=across_recv_sem.at[piece],
+            device_id=(opposite, lane),
+            device_id_type=pl.DeviceIdType.MESH,
+        )
+
+    for place in range(2):
+        for piece in range(CHUNKS):
+            hand(place, piece).start()
+            load(place, piece).start()
     for slot, (moment, _) in enumerate(plan.slots):
         source = (first_ref, second_ref)[moment]
 
@@ -86,6 +135,40 @@
         )
         when(exists, own.start)
         lax.fori_loop(1, groups * shards, send, 0)
+        if slot == 0:
+            for piece in range(CHUNKS):
+                load(0, piece).wait()
+                hand(0, piece).wait()
+
+                def add(block, carry, piece=piece):
+                    rows = pl.ds(pl.multiple_of(piece * chunk + block * BLOCK, BLOCK), BLOCK)
+                    total = mine_ref[0, rows, :].astype(jnp.float32) + pair_ref[0, rows, :].astype(jnp.float32)
+                    across_ref[rows, :] = total.astype(jnp.bfloat16)
+                    return carry
+
+                lax.fori_loop(0, chunk // BLOCK, add, 0)
+                if piece:
+                    cross(piece - 1).start()
+            for piece in range(CHUNKS):
+                load(1, piece).wait()
+                hand(1, piece).wait()
+            cross(CHUNKS - 1).start()
+    squares = jnp.zeros((1, LANES), jnp.float32)
+    for piece in range(CHUNKS):
+        cross(piece).wait()
+
+        def finish_sum(block, squares, piece=piece):
+            rows = pl.ds(pl.multiple_of(piece * chunk + block * BLOCK, BLOCK), BLOCK)
+            total = mine_ref[1, rows, :].astype(jnp.float32) + pair_ref[1, rows, :].astype(jnp.float32)
+            total = total + landed_ref[rows, :].astype(jnp.float32)
+            summed_ref[rows, :] = total
+            down = jnp.sum(total * total, axis=0, keepdims=True)
+            for tile in range(plan.tiles):
+                squares = squares + down[:, tile * LANES : (tile + 1) * LANES]
+            return squares
+
+        squares = lax.fori_loop(0, chunk // BLOCK, finish_sum, squares)
+    square_ref[...] = jnp.broadcast_to(squares, square_ref.shape)
     for slot in range(len(plan.slots)):
         tile, exists = plan.place(slot, group, lane)
         arrived = middle_ref.at[slot, pl.ds(0, (groups * shards - 1) * zero_rows), :]
@@ -105,9 +188,29 @@
         when(exists, finish)
 
 
-def deliver_kernel(plan, rows_local, ordered_ref, first_ref, second_ref, send_sem, recv_sem, own_sem):
+def deliver_kernel(
+    plan, rows_local, ordered_ref, square_ref, first_ref, second_ref, total_ref, square_all_ref,
+    send_sem, recv_sem, own_sem, square_send_sem, square_recv_sem, square_own_sem,
+):
     group, lane = lax.axis_index("group"), lax.axis_index("dp")
-    shards = plan.shards
+    groups, shards = plan.groups, plan.shards
+    count = groups * shards
+    place = square_all_ref.at[group * shards + lane]
+    own_square = pltpu.make_async_copy(square_ref, place, square_own_sem)
+    own_square.start()
+
+    def tell(step, carry):
+        pltpu.make_async_remote_copy(
+            src_ref=square_ref,
+            dst_ref=place,
+            send_sem=square_send_sem,
+            recv_sem=square_recv_sem,
+            device_id=(lax.rem(group + lax.rem(step, groups), groups), lax.rem(lane + step // groups, shards)),
+            device_id_type=pl.DeviceIdType.MESH,
+        ).start()
+        return carry
+
+    lax.fori_loop(1, count, tell, 0)
     results = (first_ref, second_ref)
     for slot, (moment, _) in enumerate(plan.slots):
         tile, exists = plan.place(slot, group, lane)
@@ -133,6 +236,11 @@
             lax.fori_loop(1, shards, send, 0)
 
         when(exists, start_slot)
+    own_square.wait()
+    others = square_all_ref.at[pl.ds(0, count - 1)]
+    await_bytes(others, square_send_sem)
+    await_bytes(others, square_recv_sem)
+    total_ref[...] = jnp.sum(square_all_ref[...], axis=0)
     for slot, (moment, turn) in enumerate(plan.slots):
         tile, exists = plan.place(slot, group, lane)
 
@@ -152,6 +260,47 @@
             else:
                 pl.when(exists)(functools.partial(arrive, plan.full + 1))
                 pl.when(~exists)(functools.partial(arrive, plan.full))
+
+
+def order_kernel(shards, rows_local, units_ref, middle_ref, ordered_ref, plain_ref, moved_ref):
+    rows = shards * rows_local
+    slots = middle_ref.shape[0]
+
+    def widen(block, carry):
+        part = pl.ds(pl.multiple_of(block * RUN, RUN), RUN)
+        for slot in range(slots):
+            plain_ref[slot, part, :] = middle_ref[slot, part, :].astype(jnp.float32)
+        return carry
+
+    lax.fori_loop(0, rows // RUN, widen, 0)
+
+    def one_lane(lane, carry):
+        offset = jnp.int32(0)
+        for param in range(units_ref.shape[0]):
+            units = units_ref[param]
+            source = shards * offset + lane * units
+            target = lane * rows_local + offset
+
+            def move(block, carry, source=source, target=target):
+                for slot in range(slots):
+                    moved_ref[slot, pl.ds(target + block * RUN, RUN), :] = plain_ref[
+                        slot, pl.ds(source + block * RUN, RUN), :
+                    ]
+                return carry
+
+            lax.fori_loop(0, (units + RUN - 1) // RUN, move, 0)
+            offset = offset + units
+        return carry
+
+    lax.fori_loop(0, shards, one_lane, 0)
+
+    def narrow(block, carry):
+        part = pl.ds(pl.multiple_of(block * RUN, RUN), RUN)
+        for slot in range(slots):
+            ordered_ref[slot, part, :] = moved_ref[slot, part, :].astype(jnp.bfloat16)
+        return carry
+
+    lax.fori_loop(0, rows // RUN, narrow, 0)
 
 
 def local(param_units, first_moment, second_moment, grad_parts, weights):
@@ -166,51 +315,59 @@
     anywhere = pl.BlockSpec(memory_space=pl.ANY)
     in_vmem = pl.BlockSpec(memory_space=pltpu.VMEM)
 
-    summed = lax.psum_scatter(
-        grad_parts.astype(jnp.float32).astype(jnp.bfloat16),
-        "group",
-        scatter_dimension=2,
-        tiled=True,
-    ).astype(jnp.float32)[0]
-    square_sum = lax.psum(jnp.sum(summed * summed), ("group", "dp"))
-    grad_rms = jnp.sqrt(square_sum / float(rows * width_full))
-    clipped = summed / jnp.maximum(grad_rms, 1.0)
-
-    middle = pl.pallas_call(
+    dma = pltpu.SemaphoreType.DMA
+    piece = (rows_local, width_part)
+    middle, summed, squares = pl.pallas_call(
         functools.partial(spread_kernel, plan, zero_rows, width_part),
+        out_shape=[
+            jax.ShapeDtypeStruct((slots, rows, LANES), jnp.bfloat16),
+            jax.ShapeDtypeStruct(piece, jnp.float32),
+            jax.ShapeDtypeStruct((8, LANES), jnp.float32),
+        ],
+        in_specs=[anywhere] * 3,
+        out_specs=[anywhere, in_vmem, in_vmem],
+        scratch_shapes=[
+            pltpu.VMEM((2, *piece), jnp.bfloat16),
+            pltpu.VMEM((2, *piece), jnp.bfloat16),
+            pltpu.VMEM(piece, jnp.bfloat16),
+            pltpu.VMEM(piece, jnp.bfloat16),
+        ]
+        + [dma((slots,))] * 3
+        + [dma((2, CHUNKS))] * 3
+        + [dma((CHUNKS,))] * 2,
+        compiler_params=pltpu.CompilerParams(has_side_effects=True),
+        name="spread",
+    )(first_moment, second_moment, grad_parts)
+
+    ordered = pl.pallas_call(
+        functools.partial(order_kernel, shards, rows_local),
         out_shape=jax.ShapeDtypeStruct((slots, rows, LANES), jnp.bfloat16),
-        in_specs=[anywhere, anywhere],
-        out_specs=anywhere,
-        scratch_shapes=[pltpu.SemaphoreType.DMA((slots,))] * 3,
-        compiler_params=pltpu.CompilerParams(has_side_effects=True),
-        cost_estimate=pl.CostEstimate(flops=0, bytes_accessed=60_000_000, transcendentals=0),
-        name="spread",
-    )(first_moment, second_moment)
-
-    offsets = jnp.cumsum(param_units) - param_units
-    local_rows = jnp.arange(rows_local, dtype=jnp.int32)
-    owners = jnp.sum(local_rows[:, None] >= (offsets + param_units)[None, :], axis=1)
-    choose = owners[:, None] == jnp.arange(param_units.shape[0])[None, :]
-    row_units = jnp.sum(jnp.where(choose, param_units, 0), axis=1)
-    row_offsets = jnp.sum(jnp.where(choose, offsets, 0), axis=1)
-    lanes = jnp.arange(shards, dtype=jnp.int32)[:, None]
-    source = (shards * row_offsets + lanes * row_units + local_rows - row_offsets).reshape(rows)
-    ordered = jnp.take(middle, source, axis=1, mode="clip")
-
-    first_rows, second_rows = pl.pallas_call(
+        in_specs=[pl.BlockSpec(memory_space=pltpu.SMEM), in_vmem],
+        out_specs=in_vmem,
+        scratch_shapes=[pltpu.VMEM((slots, rows + RUN, LANES), jnp.float32)] * 2,
+        name="order",
+    )(param_units, middle)
+
+    first_rows, second_rows, square_sums = pl.pallas_call(
         functools.partial(deliver_kernel, plan, rows_local),
-        out_shape=[jax.ShapeDtypeStruct((rows_local, width_part), jnp.bfloat16)] * 2,
-        in_specs=[anywhere],
-        out_specs=[in_vmem, in_vmem],
+        out_shape=[jax.ShapeDtypeStruct(piece, jnp.bfloat16)] * 2
+        + [jax.ShapeDtypeStruct((8, LANES), jnp.float32)],
+        in_specs=[anywhere, in_vmem],
+        out_specs=[in_vmem] * 3,
         scratch_shapes=[
-            pltpu.SemaphoreType.DMA((slots,)),
-            pltpu.SemaphoreType.DMA((2,)),
-            pltpu.SemaphoreType.DMA((slots,)),
+            pltpu.VMEM((groups * shards, 8, LANES), jnp.float32),
+            dma((slots,)),
+            dma((2,)),
+            dma((slots,)),
+            dma,
+            dma,
+            dma,
         ],
         compiler_params=pltpu.CompilerParams(has_side_effects=True),
-        cost_estimate=pl.CostEstimate(flops=0, bytes_accessed=60_000_000, transcendentals=0),
         name="deliver",
-    )(ordered)
+    )(ordered, squares)
+    grad_rms = jnp.sqrt(jnp.sum(square_sums[0]) / float(rows * width_full))
+    clipped = summed / jnp.maximum(grad_rms, 1.0)
     first_rows = first_rows.astype(jnp.float32)
     second_rows = second_rows.astype(jnp.float32)
     first_new = beta_first * first_rows + (1.0 - beta_first) * clipped

time: 234 us -> 158 us (0.68)
  blocking collectives: 41.7 us -> 0 us
  local copies, waits for them, and re-layouts: 30.2 us -> 0.01 us
  between operations: 15.9 us -> 2.48 us
  Pallas kernels: 136 us -> 148 us
    psum x1 -> x0, blocking collectives: 41.7 us -> none  [local(): square_sum = lax.psum(jnp.sum(summed * summed), ('group', 'dp'))]
    gather x2 -> x0, local copies, waits for them, and re-layouts: 25.5 us -> none  [local(): ordered = jnp.take(middle, source, axis=1, mode='clip')]
    pallas_call x0 -> x1, Pallas kernels: none -> 6.36 us  [local(): pl.pallas_call(functools.partial(order_kernel, shards, rows_local), out_s...]
    pallas_call x1 -> x0, local copies, waits for them, and re-layouts: 4.7 us -> none  [local(): pl.pallas_call(functools.partial(spread_kernel, plan, zero_rows, width_pa...]
    pallas_call x1, Pallas kernels: 66.6 us -> 69.7 us  [local(): pl.pallas_call(functools.partial(deliver_kernel, plan, rows_local), out_s...]
    pallas_call x1, Pallas kernels: 69.6 us -> 72.1 us  [local(): pl.pallas_call(functools.partial(spread_kernel, plan, zero_rows, width_pa...]
  transfers between devices with their start and end apart: 1 -> 0, of which waited for: 0 -> 0; matrix products, arithmetic and copies ran while one was open for 13% -> 0% of each run, Pallas kernels for 30% -> 0%
where the time goes in v2:
time: 158 us
  Pallas kernels  148 us (94%)
  other arithmetic  7.58 us (5%)
  between operations  2.48 us (2%)
    pallas_call x1, Pallas kernels, local(): pl.pallas_call(functools.partial(spread_kernel, plan, zero_rows, width_pa...  72.1 us
    pallas_call x1, Pallas kernels, local(): pl.pallas_call(functools.partial(deliver_kernel, plan, rows_local), out_s...  69.7 us
    pallas_call x1, Pallas kernels, local(): pl.pallas_call(functools.partial(order_kernel, shards, rows_local), out_s...  6.36 us
    add x1, other arithmetic, local(): first_new / (jnp.sqrt(second_new) + epsilon)  6.29 us

profile of v2, /device:TPU:0, one launch (start us, length us, event | category | flops | bytes accessed | tf_op | source)
XLA Modules:
  0.0 158.2 jit_solution(7524388199616949851)
XLA Ops:
  0.6 72.1 %spread.1 = (bf16[4,3072,128]{2,1,0:T(8,128)(2,1)}, f32[384,1792]{1,0:T(8,128)}, f32[8,128]{1,0:T(8,128)}) custom-call(bf16[96,7168]{1,0:T(8,128)(2,1)} %first_ref.1, bf16[96,7168]{1,0:T(8,128)(2,1)} %second_ref.1, bf16[1,384,7168]{2,1,0:T(8,128)(2,1)} %grad_ref.1), custom_call_target="tpu_custom_call" | custom-call | tf_op jit(solution)/shard_map/spread/pallas_call | solution.py:320
  72.7 6.4 %order.1.ordered_ref = bf16[4,3072,128]{2,1,0:T(8,128)(2,1)} custom-call(s32[6]{0:T(128)} %units_ref.1, bf16[4,3072,128]{2,1,0:T(8,128)(2,1)} %get-tuple-element.10.middle_ref), custom_call_target="tpu_custom_call" | custom-call | tf_op jit(solution)/shard_map/order/pallas_call | solution.py:342
  79.1 0.0 copy-start
  79.1 69.7 %deliver.1 = (bf16[384,1792]{1,0:T(8,128)(2,1)}, bf16[384,1792]{1,0:T(8,128)(2,1)}, f32[8,128]{1,0:T(8,128)}) custom-call(bf16[4,3072,128]{2,1,0:T(8,128)(2,1)} %order.1.ordered_ref, f32[8,128]{1,0:T(8,128)} %get-tuple-element.11.square_ref), custom_call_target="tpu_custom_call" | custom-call | tf_op jit(solution)/shard_map/deliver/pallas_call | solution.py:351
  148.8 1.3 slice_reduce_fusion
  150.8 0.0 copy-done
  150.8 6.3 %multiply_add_fusion = (f32[384,1792]{1,0:T(8,128)}, bf16[384,1792]{1,0:T(8,128)(2,1)}, bf16[384,1792]{1,0:T(8,128)(2,1)}) fusion(bf16[384,1792]{1,0:T(8,128)(2,1)} %param.9, bf16[384,1792]{1,0:T(8,128)(2,1)} %get-tuple-element.12, bf16[384,1792]{1,0:T(8,128)(2,1)} %get-tuple-element.15, f32[384,1792]{1,0:T(8,128)S(1)} %copy-done, f32[]{:T(128)S(6)} %max.3), kind=kLoop, calls=%fused_computation.2 | loop fusion | flops 11698176 | bytes 12386308 | tf_op jit(solution)/shard_map/add | solution.py:375
Async XLA Ops:
  79.1 71.7 %copy-start = (f32[384,1792]{1,0:T(8,128)S(1)}, f32[384,1792]{1,0:T(8,128)}, u32[]{:S(2)}) copy-start(f32[384,1792]{1,0:T(8,128)} %get-tuple-element.13) | copy-start | bytes 8257540

commit v3 on v2

v3 whole, which is shorter than its diff:
```python
import functools

import jax
import jax.numpy as jnp
from jax import lax
from jax.experimental import pallas as pl
from jax.experimental.pallas import tpu as pltpu
from jax.sharding import PartitionSpec as P

beta_first = 0.9
beta_second = 0.95
epsilon = 1e-08
decay_weight = 0.1
LANES = 128
CHUNKS = 4
BLOCK = 16
RUN = 32


class Plan:
    def __init__(self, groups, shards, tiles):
        self.groups, self.shards, self.tiles = groups, shards, tiles
        self.full, self.rest = tiles // shards, tiles % shards
        self.slots = []
        for moment in range(2):
            self.slots += [(moment, turn) for turn in range(self.full)]
            if self.rest:
                self.slots.append((moment, self.full))

    def partial(self, slot):
        return self.slots[slot][1] == self.full

    def place(self, slot, group, lane):
        moment, turn = self.slots[slot]
        if turn < self.full:
            return turn * self.shards + lane, None
        shift = (self.shards // 2) * moment + (self.shards // 4) * lax.rem(group, 2)
        rank = lax.rem(lane + shift, self.shards)
        return self.full * self.shards + jnp.minimum(rank, self.rest - 1), rank < self.rest


def when(condition, body):
    if condition is None:
        body()
    else:
        pl.when(condition)(body)


def both(first, second):
    return second if first is None else first & second


def await_bytes(ref, sem):
    pltpu.make_async_copy(ref, ref, sem).wait()


def move_kernel(
    plan, zero_rows, width_part, units_ref, first_ref, second_ref, grad_ref,
    summed_ref, total_ref, first_rows_ref, second_rows_ref,
    pair_ref, mine_ref, across_ref, landed_ref, middle_ref, ordered_ref, plain_ref, square_ref, square_all_ref,
    send_sem, recv_sem, own_sem, load_sem, pair_send_sem, pair_recv_sem, across_send_sem, across_recv_sem,
    out_send_sem, out_recv_sem, out_own_sem, square_send_sem, square_recv_sem, square_own_sem,
):
    group, lane = lax.axis_index("group"), lax.axis_index("dp")
    groups, shards = plan.groups, plan.shards
    base = (group * shards + lane) * zero_rows
    rows_local = grad_ref.shape[1]
    chunk = rows_local // CHUNKS
    core = lax.rem(group, 2)
    beside, opposite = group + 1 - 2 * core, lax.rem(group + 2, groups)

    def quarter(owner, rows):
        return grad_ref.at[0, rows, pl.ds(pl.multiple_of(owner * width_part, LANES), width_part)]

    def part(place):
        return pl.ds(place * chunk, chunk)

    def load(place, piece):
        return pltpu.make_async_copy(
            quarter((opposite, group)[place], part(piece)),
            mine_ref.at[place, part(piece), :],
            load_sem.at[place, piece],
        )

    def hand(place, piece):
        return pltpu.make_async_remote_copy(
            src_ref=quarter((lax.rem(beside + 2, groups), beside)[place], part(piece)),
            dst_ref=pair_ref.at[place, part(piece), :],
            send_sem=pair_send_sem.at[place, piece],
            recv_sem=pair_recv_sem.at[place, piece],
            device_id=(beside, lane),
            device_id_type=pl.DeviceIdType.MESH,
        )

    def cross(piece):
        return pltpu.make_async_remote_copy(
            src_ref=across_ref.at[part(piece), :],
            dst_ref=landed_ref.at[part(piece), :],
            send_sem=across_send_sem.at[piece],
            recv_sem=across_recv_sem.at[piece],
            device_id=(opposite, lane),
            device_id_type=pl.DeviceIdType.MESH,
        )

    for place in range(2):
        for piece in range(CHUNKS):
            hand(place, piece).start()
            load(place, piece).start()
    for slot, (moment, _) in enumerate(plan.slots):
        source = (first_ref, second_ref)[moment]

        def send(step, carry, slot=slot, source=source):
            to_group = lax.rem(group + lax.rem(step, groups), groups)
            to_lane = lax.rem(lane + step // groups, shards)
            tile, exists = plan.place(slot, to_group, to_lane)
            column = pl.multiple_of(to_group * width_part + tile * LANES, LANES)

            def start():
                pltpu.make_async_remote_copy(
                    src_ref=source.at[:, pl.ds(column, LANES)],
                    dst_ref=middle_ref.at[slot, pl.ds(base, zero_rows), :],
                    send_sem=send_sem.at[slot],
                    recv_sem=recv_sem.at[slot],
                    device_id=(to_group, to_lane),
                    device_id_type=pl.DeviceIdType.MESH,
                ).start()

            when(exists, start)
            return carry

        tile, exists = plan.place(slot, group, lane)
        column = pl.multiple_of(group * width_part + tile * LANES, LANES)
        own = pltpu.make_async_copy(
            source.at[:, pl.ds(column, LANES)],
            middle_ref.at[slot, pl.ds(base, zero_rows), :],
            own_sem.at[slot],
        )
        when(exists, own.start)
        lax.fori_loop(1, groups * shards, send, 0)
        if slot == 0:
            for piece in range(CHUNKS):
                load(0, piece).wait()
                hand(0, piece).wait()

                def add(block, carry, piece=piece):
                    rows = pl.ds(pl.multiple_of(piece * chunk + block * BLOCK, BLOCK), BLOCK)
                    total = mine_ref[0, rows, :].astype(jnp.float32) + pair_ref[0, rows, :].astype(jnp.float32)
                    across_ref[rows, :] = total.astype(jnp.bfloat16)
                    return carry

                lax.fori_loop(0, chunk // BLOCK, add, 0)
                if piece:
                    cross(piece - 1).start()
            for piece in range(CHUNKS):
                load(1, piece).wait()
                hand(1, piece).wait()
            cross(CHUNKS - 1).start()

    results = (first_rows_ref, second_rows_ref)
    rows = shards * rows_local

    def put_in_order(slot):
        def widen(block, carry):
            part = pl.multiple_of(block * RUN, RUN)
            plain_ref[pl.ds(pl.multiple_of(part + BLOCK, BLOCK), RUN), :] = middle_ref[
                slot, pl.ds(part, RUN), :
            ].astype(jnp.float32)
            return carry

        lax.fori_loop(0, rows // RUN, widen, 0)

        def gather(block, carry):
            begin = pl.multiple_of(block * BLOCK, BLOCK)
            to_lane = begin // rows_local
            within = begin - to_lane * rows_local
            index = lax.broadcasted_iota(jnp.int32, (BLOCK, LANES), 0) + within
            offset = jnp.int32(0)
            value = jnp.zeros((BLOCK, LANES), jnp.float32)
            for param in range(units_ref.shape[0]):
                units = units_ref[param]
                source = shards * offset + to_lane * units + within - offset
                source = jnp.clip(source + BLOCK, 0, rows + BLOCK)
                value = jnp.where(index >= offset, plain_ref[pl.ds(source, BLOCK), :], value)
                offset = offset + units
            ordered_ref[slot, pl.ds(begin, BLOCK), :] = value.astype(jnp.bfloat16)
            return carry

        lax.fori_loop(0, rows // BLOCK, gather, 0)

    def pass_on(slot, moment, tile):
        target = results[moment].at[:, pl.ds(pl.multiple_of(tile * LANES, LANES), LANES)]
        pltpu.make_async_copy(
            ordered_ref.at[slot, pl.ds(pl.multiple_of(lane * rows_local, BLOCK), rows_local), :],
            target,
            out_own_sem.at[slot],
        ).start()

        def send(step, carry):
            to_lane = lax.rem(lane + step, shards)
            pltpu.make_async_remote_copy(
                src_ref=ordered_ref.at[slot, pl.ds(pl.multiple_of(to_lane * rows_local, BLOCK), rows_local), :],
                dst_ref=target,
                send_sem=out_send_sem.at[slot],
                recv_sem=out_recv_sem.at[moment],
                device_id=(group, to_lane),
                device_id_type=pl.DeviceIdType.MESH,
            ).start()
            return carry

        lax.fori_loop(1, shards, send, 0)

    def sum_up():
        squares = jnp.zeros((1, LANES), jnp.float32)
        for piece in range(CHUNKS):
            cross(piece).wait()

            def finish_sum(block, squares, piece=piece):
                rows = pl.ds(pl.multiple_of(piece * chunk + block * BLOCK, BLOCK), BLOCK)
                total = mine_ref[1, rows, :].astype(jnp.float32) + pair_ref[1, rows, :].astype(jnp.float32)
                total = total + landed_ref[rows, :].astype(jnp.float32)
                summed_ref[rows, :] = total
                down = jnp.sum(total * total, axis=0, keepdims=True)
                for tile in range(plan.tiles):
                    squares = squares + down[:, tile * LANES : (tile + 1) * LANES]
                return squares

            squares = lax.fori_loop(0, chunk // BLOCK, finish_sum, squares)
        square_ref[...] = jnp.broadcast_to(squares, square_ref.shape)

    count = groups * shards
    place = square_all_ref.at[group * shards + lane]

    def tell_squares():
        pltpu.make_async_copy(square_ref, place, square_own_sem).start()

        def tell(step, carry):
            pltpu.make_async_remote_copy(
                src_ref=square_ref,
                dst_ref=place,
                send_sem=square_send_sem,
                recv_sem=square_recv_sem,
                device_id=(lax.rem(group + lax.rem(step, groups), groups), lax.rem(lane + step // groups, shards)),
                device_id_type=pl.DeviceIdType.MESH,
            ).start()
            return carry

        lax.fori_loop(1, count, tell, 0)

    last = len(plan.slots) - 1
    for slot, (moment, _) in enumerate(plan.slots):
        if slot == last:
            sum_up()
        tile, exists = plan.place(slot, group, lane)

        def handle(slot=slot, moment=moment, tile=tile):
            await_bytes(middle_ref.at[slot, pl.ds(0, (count - 1) * zero_rows), :], recv_sem.at[slot])
            await_bytes(middle_ref.at[slot, pl.ds(0, zero_rows), :], own_sem.at[slot])
            put_in_order(slot)
            pass_on(slot, moment, tile)

        when(exists, handle)
        if slot == last:
            tell_squares()

    for slot, (moment, _) in enumerate(plan.slots):
        tile, exists = plan.place(slot, group, lane)
        if exists is None:
            await_bytes(middle_ref.at[slot, pl.ds(0, (count - 1) * zero_rows), :], send_sem.at[slot])
        else:
            others = groups * plan.rest
            less = middle_ref.at[slot, pl.ds(0, (others - 1) * zero_rows), :]
            more = middle_ref.at[slot, pl.ds(0, others * zero_rows), :]
            pl.when(exists)(functools.partial(await_bytes, less, send_sem.at[slot]))
            pl.when(~exists)(functools.partial(await_bytes, more, send_sem.at[slot]))

        def finish_slot(slot=slot):
            await_bytes(ordered_ref.at[slot, pl.ds(0, (shards - 1) * rows_local), :], out_send_sem.at[slot])
            await_bytes(ordered_ref.at[slot, pl.ds(0, rows_local), :], out_own_sem.at[slot])

        when(exists, finish_slot)
        if slot == last or plan.slots[slot + 1][0] != moment:
            result = results[moment]

            def arrive(own, result=result, moment=moment):
                await_bytes(result.at[:, pl.ds(0, (plan.tiles - own) * LANES)], out_recv_sem.at[moment])

            if exists is None:
                arrive(plan.full)
            else:
                pl.when(exists)(functools.partial(arrive, plan.full + 1))
                pl.when(~exists)(functools.partial(arrive, plan.full))
    await_bytes(place, square_own_sem)
    others = square_all_ref.at[pl.ds(0, count - 1)]
    await_bytes(others, square_send_sem)
    await_bytes(others, square_recv_sem)
    total_ref[...] = jnp.sum(square_all_ref[...], axis=0)


def local(param_units, first_moment, second_moment, grad_parts, weights):
    groups = lax.axis_size("group")
    shards = lax.axis_size("dp")
    rows_local, width_part = weights.shape
    width_full = grad_parts.shape[2]
    zero_rows = first_moment.shape[0]
    rows = rows_local * shards
    plan = Plan(groups, shards, width_part // LANES)
    slots = len(plan.slots)
    anywhere = pl.BlockSpec(memory_space=pl.ANY)
    in_vmem = pl.BlockSpec(memory_space=pltpu.VMEM)

    dma = pltpu.SemaphoreType.DMA
    piece = (rows_local, width_part)
    summed, square_sums, first_rows, second_rows = pl.pallas_call(
        functools.partial(move_kernel, plan, zero_rows, width_part),
        out_shape=[
            jax.ShapeDtypeStruct(piece, jnp.float32),
            jax.ShapeDtypeStruct((8, LANES), jnp.float32),
            jax.ShapeDtypeStruct(piece, jnp.bfloat16),
            jax.ShapeDtypeStruct(piece, jnp.bfloat16),
        ],
        in_specs=[pl.BlockSpec(memory_space=pltpu.SMEM)] + [anywhere] * 3,
        out_specs=[in_vmem] * 4,
        scratch_shapes=[
            pltpu.VMEM((2, *piece), jnp.bfloat16),
            pltpu.VMEM((2, *piece), jnp.bfloat16),
            pltpu.VMEM(piece, jnp.bfloat16),
            pltpu.VMEM(piece, jnp.bfloat16),
            pltpu.VMEM((slots, rows, LANES), jnp.bfloat16),
            pltpu.VMEM((slots, rows, LANES), jnp.bfloat16),
            pltpu.VMEM((rows + 2 * BLOCK, LANES), jnp.float32),
            pltpu.VMEM((8, LANES), jnp.float32),
            pltpu.VMEM((groups * shards, 8, LANES), jnp.float32),
        ]
        + [dma((slots,))] * 3
        + [dma((2, CHUNKS))] * 3
        + [dma((CHUNKS,))] * 2
        + [dma((slots,)), dma((2,)), dma((slots,)), dma, dma, dma],
        compiler_params=pltpu.CompilerParams(has_side_effects=True),
        name="move",
    )(param_units, first_moment, second_moment, grad_parts)
    grad_rms = jnp.sqrt(jnp.sum(square_sums[0]) / float(rows * width_full))
    clipped = summed / jnp.maximum(grad_rms, 1.0)
    first_rows = first_rows.astype(jnp.float32)
    second_rows = second_rows.astype(jnp.float32)
    first_new = beta_first * first_rows + (1.0 - beta_first) * clipped
    second_new = beta_second * second_rows + (1.0 - beta_second) * clipped * clipped
    direction = first_new / (jnp.sqrt(second_new) + epsilon) + decay_weight * weights.astype(
        jnp.float32
    )
    return (first_new.astype(jnp.bfloat16), second_new.astype(jnp.bfloat16), direction, grad_rms)


def solution(mesh):
    in_specs = (
        P(),
        P(("group", "dp"), None),
        P(("group", "dp"), None),
        P("group", "dp", None),
        P("dp", "group"),
    )
    out_specs = (P("dp", "group"), P("dp", "group"), P("dp", "group"), P())
    return jax.shard_map(local, mesh=mesh, in_specs=in_specs, out_specs=out_specs, check_vma=False)
```

time: 158 us -> 148 us (0.937)
  Pallas kernels: 148 us -> 138 us
    pallas_call x3 -> x1, Pallas kernels: 148 us -> 138 us  [local(): pl.pallas_call(functools.partial(move_kernel, plan, zero_rows, width_part...]
where the time goes in v3:
time: 148 us
  Pallas kernels  138 us (93%)
  other arithmetic  8.02 us (5%)
  between operations  2.48 us (2%)
    pallas_call x1, Pallas kernels, local(): pl.pallas_call(functools.partial(move_kernel, plan, zero_rows, width_part...  138 us
    add x1, other arithmetic, local(): first_new / (jnp.sqrt(second_new) + epsilon)  6.74 us

profile of v3, /device:TPU:0, one launch (start us, length us, event | category | flops | bytes accessed | tf_op | source)
XLA Modules:
  0.0 148.0 jit_solution(12223539696901489752)
XLA Ops:
  0.6 0.0 copy-start
  0.6 137.5 %move.1 = (f32[384,1792]{1,0:T(8,128)}, f32[8,128]{1,0:T(8,128)}, bf16[384,1792]{1,0:T(8,128)(2,1)}, bf16[384,1792]{1,0:T(8,128)(2,1)}) custom-call(s32[6]{0:T(128)} %units_ref.1, bf16[96,7168]{1,0:T(8,128)(2,1)} %first_ref.1, bf16[96,7168]{1,0:T(8,128)(2,1)} %second_ref.1, bf16[1,384,7168]{2,1,0:T(8,128)(2,1)} %grad_ref.1), custom_call_target="tpu_custom_call" | custom-call | tf_op jit(solution)/shard_map/move/pallas_call | solution.py:313
  138.2 1.3 slice_reduce_fusion
  140.2 0.0 copy-done
  140.2 6.7 %multiply_add_fusion = (f32[384,1792]{1,0:T(8,128)}, bf16[384,1792]{1,0:T(8,128)(2,1)}, bf16[384,1792]{1,0:T(8,128)(2,1)}) fusion(bf16[384,1792]{1,0:T(8,128)(2,1)S(1)} %copy-done, bf16[384,1792]{1,0:T(8,128)(2,1)} %get-tuple-element.8, bf16[384,1792]{1,0:T(8,128)(2,1)} %get-tuple-element.11, f32[384,1792]{1,0:T(8,128)} %get-tuple-element.9, f32[]{:T(128)S(6)} %max.3), kind=kLoop, calls=%fused_computation.2 | loop fusion | flops 11698176 | bytes 12386308 | tf_op jit(solution)/shard_map/add | solution.py:347
Async XLA Ops:
  0.6 139.5 %copy-start = (bf16[384,1792]{1,0:T(8,128)(2,1)S(1)}, bf16[384,1792]{1,0:T(8,128)(2,1)}, u32[]{:S(2)}) copy-start(bf16[384,1792]{1,0:T(8,128)(2,1)} %param.9) | copy-start | bytes 4128772
